TPU v7x, 32 devices: a whole 2x2x4 slice. The times are simulated.
32 devices in a mesh: bl: 8 (over y, x, core), bp: 4 (over z).
Axes of the slice: x: 2, y: 2, z: 4, core: 2. Of those that a mesh axis runs over, the one named last changes fastest.
Arguments:
- inverse_cov: float32 [8, 1024, 1024], P('bl', 'bp'), may hold values from -1 to 12, as said below
- channel_keep_mask: int32 [8, 1024], P('bl'), may hold values 0 or 1
- partner_ids: int32 [8, 2], P('bl'), may hold values from -1 to 7, as said below
- band_starts: int32 [2, 64], replicated, may hold values from 0 to 384
Outputs:
- fisher: float32 [2, 64, 64], P(None, 'bp', 'bl')
Inputs may be any that keep to these rules, and one draw needn't show every extreme that they name: partner_ids[i, k] is -1 for an empty slot, else the index of a baseline whose group, its index // 1, lies 1 to 4 groups after the group of baseline i, counted cyclically over the 8 groups; in every draw some baseline has all 2 slots filled. Each inverse_cov[i] is symmetric.
All inputs are finite; a program needn't handle non-finite values. No bound on the sum of `channel_keep_mask` on one device may be relied on, other than what follows from the above.
Results may differ from a plain program's by a relative error of at most 0.0003.
Values sent between devices are 32-bit elements; how exact they have to be, the bound alone decides.
A program may use at most 128 MiB of HBM per device.

v0:
```python
from functools import partial

import jax
import jax.numpy as jnp
from jax import lax
from jax.sharding import PartitionSpec as P

WINDOW_LENGTH = 128
GROUP_REACH = 4


highest = lax.Precision.HIGHEST


def passed_along(value, axis, steps):
    count = lax.axis_size(axis)
    pairs = [(source, (source + steps) % count) for source in range(count)]
    return lax.ppermute(value, axis, pairs)


def kernel_stack(first_band, band_count, window):
    channel_pos = jnp.arange(window, dtype=jnp.float32)
    spread = jnp.abs(channel_pos[:, None] - channel_pos[None, :])
    band_ids = first_band + jnp.arange(band_count, dtype=jnp.int32)
    length = 1.0 + (band_ids % 4).astype(jnp.float32)
    return jnp.exp(-spread[None, :, :] / length[:, None, None])


def project_turned(panel_block, starts, kernels):
    window = kernels.shape[1]
    window_rows = jax.vmap(
        lambda row_start: lax.dynamic_slice_in_dim(panel_block, row_start, window, 0)
    )(starts)
    return jnp.einsum(
        "apq,aqc->acp", kernels, window_rows, precision=highest, preferred_element_type=jnp.float32
    )


def row_windows(turned, starts, window):

    def one_matrix(matrix):
        return jax.vmap(lambda row_start: lax.dynamic_slice_in_dim(matrix, row_start, window, 0))(
            starts
        )

    return jax.vmap(one_matrix)(turned)


def take_member(received, team_element):
    return lax.dynamic_index_in_dim(received, team_element, 0, keepdims=False)


def contract(turned, block_starts, own_windows):
    partner_windows = row_windows(turned, block_starts, own_windows.shape[2])
    return jnp.einsum(
        "abqp,bapq->ab",
        partner_windows,
        own_windows,
        precision=highest,
        preferred_element_type=jnp.float32,
    )


def block_step(
    block_idx, own_panel, all_start, all_kernels, my_start, projections, presence, block_width
):
    block_begin = block_idx * block_width
    block_starts = lax.dynamic_slice_in_dim(all_start, block_begin, block_width)
    block_kernels = lax.dynamic_slice_in_dim(all_kernels, block_begin, block_width)
    own_turned = project_turned(own_panel, block_starts, block_kernels)
    own_windows = row_windows(own_turned, my_start, all_kernels.shape[1])
    column_sum = jnp.zeros((my_start.shape[0], block_width), jnp.float32)
    for projected, present in zip(projections, presence):
        column_sum = column_sum + lax.cond(
            present,
            partial(contract, projected, block_starts, own_windows),
            partial(jnp.zeros, (my_start.shape[0], block_width), jnp.float32),
        )
    return column_sum


def body(inverse_cov, channel_keep_mask, partner_ids, band_starts):
    local_count, shard_rows, channels = inverse_cov.shape
    panel_width = channels // 2
    window = WINDOW_LENGTH
    band_total = band_starts.shape[1]
    antenna_pair_sets = lax.axis_size("bl")
    owners = lax.axis_size("bp")
    cycle_index = lax.axis_index("bl")
    band_share = band_total // owners
    first_band = lax.axis_index("bp") * band_share
    row_first = lax.axis_index("bp") * shard_rows
    half_start = row_first // panel_width * panel_width
    flag_marks = channel_keep_mask.astype(jnp.float32)
    block_part = lax.dynamic_slice_in_dim(inverse_cov, half_start, panel_width, 2)
    row_marks = lax.dynamic_slice_in_dim(flag_marks, row_first, shard_rows, 1)
    column_marks = lax.dynamic_slice_in_dim(flag_marks, half_start, panel_width, 1)
    masked = block_part * row_marks[:, :, None] * column_marks[:, None, :]
    full_shape = (local_count, 2, panel_width, panel_width)
    own_panels = lax.all_gather(masked, "bp", axis=1, tiled=True).reshape(full_shape)
    arrived = [
        passed_along(own_panels, "bl", -number_of_hops)
        for number_of_hops in range(1, GROUP_REACH + 1)
    ]
    pickers = [partial(take_member, received) for received in arrived]
    my_kernels = kernel_stack(first_band, band_share, window)
    all_kernels = kernel_stack(0, band_total, window)
    block_width = 4
    block_count = band_total // block_width
    halves = [jnp.zeros((band_share, band_total), jnp.float32) for half_index in range(2)]
    targets = partner_ids[0]
    presence_all = targets >= 0
    hop_index = jnp.clip(
        (targets // local_count - cycle_index) % antenna_pair_sets - 1, 0, GROUP_REACH - 1
    )
    team_element = jnp.clip(targets % local_count, 0, local_count - 1)
    summed_panels = jnp.zeros((2, panel_width, panel_width), jnp.float32)
    for slot_index in range(targets.shape[0]):
        summed_panels = summed_panels + jnp.where(
            presence_all[slot_index],
            lax.switch(hop_index[slot_index], pickers, team_element[slot_index]),
            0.0,
        )
    for half_index in range(2):
        all_start = band_starts[half_index]
        my_start = lax.dynamic_slice_in_dim(all_start, first_band, band_share)
        projections = [project_turned(summed_panels[half_index], my_start, my_kernels)]
        presence = [jnp.any(presence_all)]
        stepper = partial(
            block_step,
            own_panel=own_panels[0, half_index],
            all_start=all_start,
            all_kernels=all_kernels,
            my_start=my_start,
            projections=projections,
            presence=presence,
            block_width=block_width,
        )
        block_sums = lax.map(stepper, jnp.arange(block_count, dtype=jnp.int32))
        running_totals = jnp.transpose(block_sums, (1, 0, 2)).reshape(band_share, band_total)
        halves[half_index] = halves[half_index] + running_totals
    normalizer = 1.0 / (4 * local_count * antenna_pair_sets * window)
    partial_fisher = jnp.stack(halves) * normalizer
    return lax.psum_scatter(partial_fisher, "bl", scatter_dimension=2, tiled=True)


def solution(mesh):
    placed = (P("bl", "bp", None), P("bl", None), P("bl", None), P())
    return jax.shard_map(
        body, mesh=mesh, in_specs=placed, out_specs=P(None, "bp", "bl"), check_vma=False
    )
```

profile of v0, /device:TPU:0, one launch (start us, length us, event | category | flops | bytes accessed | tf_op | source)
XLA Modules:
  0.0 1345.0 jit_solution(11537821896451937331)
XLA Ops:
  9.2 48.5 %all-gather.2.cloned.1.call-done = f32[1,1024,512]{2,1,0:T(8,128)} async-done(((f32[1,256,512]{2,1,0:T(8,128)}), f32[1,1024,512]{2,1,0:T(8,128)}) %all-gather.2.cloned.1.call-update) | async-done | bytes 2097168 | tf_op jit(solution)/shard_map/all_gather | solution.py:100
  73.4 32.1 %collective-permute-done = f32[1,2,512,512]{3,2,1,0:T(8,128)} collective-permute-done((f32[1,2,512,512]{3,2,1,0:T(8,128)}, f32[1,2,512,512]{3,2,1,0:T(8,128)}, u32[]{:S(2)}, u32[]{:S(2)}) %collective-permute-start) | collective-permute-done | bytes 2097184 | tf_op jit(solution)/shard_map/ppermute | solution.py:18
  105.5 45.2 %collective-permute-done.1 = f32[1,2,512,512]{3,2,1,0:T(8,128)S(1)} collective-permute-done((f32[1,2,512,512]{3,2,1,0:T(8,128)}, f32[1,2,512,512]{3,2,1,0:T(8,128)S(1)}, u32[]{:S(2)}, u32[]{:S(2)}) %collective-permute-start.1) | collective-permute-done | bytes 2097184 | tf_op jit(solution)/shard_map/ppermute | solution.py:18
  164.3 33.6 %while.30 = (s32[]{:T(128)}, f32[512,512]{1,0:T(8,128)S(1)}, s32[16,2]{0,1:T(2,128)S(1)}, f32[16,128,512]{2,1,0:T(8,128)}, s32[]{:T(128)}) while((s32[]{:T(128)}, f32[512,512]{1,0:T(8,128)S(1)}, s32[16,2]{0,1:T(2,128)S(1)}, f32[16,128,512]{2,1,0:T(8,128)}, s32[]{:T(128)}) %tuple.227), condition=%wide.while_cond.2, body=%wide.while_body.2.sunk | while | flops 2 | bytes 525401 | solution.py:32
  197.8 8.6 fusion.17
  210.9 518.8 %while.27 = (s32[]{:T(128)}, f32[16,16,4]{1,2,0:T(4,128)S(1)}, pred[]{:T(512)}, s32[16]{0:T(128)S(1)}, s32[64]{0:T(128)S(1)}, /*index=5*/f32[512,512]{1,0:T(8,12...) while((s32[]{:T(128)}, f32[16,16,4]{1,2,0:T(4,128)S(1)}, ...), condition=%wide.region_12.13_spmd, body=%wide.region_9.12_spmd.sunk | while | flops 404750400 | bytes 38540844 | solution.py:139
  212.3 8.5 while.32
  224.2 19.3 %conditional.8 = (f32[1,16,4]{1,2,0:T(4,128)S(1)}) conditional(s32[]{:T(128)} %convert_element_type.36, () %tuple.203, (s32[4]{0:T(128)S(1)}, f32[16,512,128]{2,0,1:T(8,128)}, s32[16]{0:T(128)S(1)}, f32[4,512,128]{2,1,0:T(8,128)S(1)}) %tuple.205), branch_computations={%region_10.10_spmd, %region_11.11_spmd} | conditional | flops 2097188 | bytes 35652680 | solution.py:74
  244.7 8.5 while.32
  256.6 19.3 %conditional.8 = (f32[1,16,4]{1,2,0:T(4,128)S(1)}) conditional(s32[]{:T(128)} %convert_element_type.36, () %tuple.203, (s32[4]{0:T(128)S(1)}, f32[16,512,128]{2,0,1:T(8,128)}, s32[16]{0:T(128)S(1)}, f32[4,512,128]{2,1,0:T(8,128)S(1)}) %tuple.205), branch_computations={%region_10.10_spmd, %region_11.11_spmd} | conditional | flops 2097188 | bytes 35652680 | solution.py:74
  277.1 8.5 while.32
  289.0 19.3 %conditional.8 = (f32[1,16,4]{1,2,0:T(4,128)S(1)}) conditional(s32[]{:T(128)} %convert_element_type.36, () %tuple.203, (s32[4]{0:T(128)S(1)}, f32[16,512,128]{2,0,1:T(8,128)}, s32[16]{0:T(128)S(1)}, f32[4,512,128]{2,1,0:T(8,128)S(1)}) %tuple.205), branch_computations={%region_10.10_spmd, %region_11.11_spmd} | conditional | flops 2097188 | bytes 35652680 | solution.py:74
  309.5 8.5 while.32
  321.4 19.3 %conditional.8 = (f32[1,16,4]{1,2,0:T(4,128)S(1)}) conditional(s32[]{:T(128)} %convert_element_type.36, () %tuple.203, (s32[4]{0:T(128)S(1)}, f32[16,512,128]{2,0,1:T(8,128)}, s32[16]{0:T(128)S(1)}, f32[4,512,128]{2,1,0:T(8,128)S(1)}) %tuple.205), branch_computations={%region_10.10_spmd, %region_11.11_spmd} | conditional | flops 2097188 | bytes 35652680 | solution.py:74
  353.8 19.3 %conditional.8 = (f32[1,16,4]{1,2,0:T(4,128)S(1)}) conditional(s32[]{:T(128)} %convert_element_type.36, () %tuple.203, (s32[4]{0:T(128)S(1)}, f32[16,512,128]{2,0,1:T(8,128)}, s32[16]{0:T(128)S(1)}, f32[4,512,128]{2,1,0:T(8,128)S(1)}) %tuple.205), branch_computations={%region_10.10_spmd, %region_11.11_spmd} | conditional | flops 2097188 | bytes 35652680 | solution.py:74
  374.3 8.5 while.32
  386.3 19.3 %conditional.8 = (f32[1,16,4]{1,2,0:T(4,128)S(1)}) conditional(s32[]{:T(128)} %convert_element_type.36, () %tuple.203, (s32[4]{0:T(128)S(1)}, f32[16,512,128]{2,0,1:T(8,128)}, s32[16]{0:T(128)S(1)}, f32[4,512,128]{2,1,0:T(8,128)S(1)}) %tuple.205), branch_computations={%region_10.10_spmd, %region_11.11_spmd} | conditional | flops 2097188 | bytes 35652680 | solution.py:74
  406.8 8.5 while.32
  418.7 19.3 %conditional.8 = (f32[1,16,4]{1,2,0:T(4,128)S(1)}) conditional(s32[]{:T(128)} %convert_element_type.36, () %tuple.203, (s32[4]{0:T(128)S(1)}, f32[16,512,128]{2,0,1:T(8,128)}, s32[16]{0:T(128)S(1)}, f32[4,512,128]{2,1,0:T(8,128)S(1)}) %tuple.205), branch_computations={%region_10.10_spmd, %region_11.11_spmd} | conditional | flops 2097188 | bytes 35652680 | solution.py:74
  451.1 19.3 %conditional.8 = (f32[1,16,4]{1,2,0:T(4,128)S(1)}) conditional(s32[]{:T(128)} %convert_element_type.36, () %tuple.203, (s32[4]{0:T(128)S(1)}, f32[16,512,128]{2,0,1:T(8,128)}, s32[16]{0:T(128)S(1)}, f32[4,512,128]{2,1,0:T(8,128)S(1)}) %tuple.205), branch_computations={%region_10.10_spmd, %region_11.11_spmd} | conditional | flops 2097188 | bytes 35652680 | solution.py:74
  483.5 19.3 %conditional.8 = (f32[1,16,4]{1,2,0:T(4,128)S(1)}) conditional(s32[]{:T(128)} %convert_element_type.36, () %tuple.203, (s32[4]{0:T(128)S(1)}, f32[16,512,128]{2,0,1:T(8,128)}, s32[16]{0:T(128)S(1)}, f32[4,512,128]{2,1,0:T(8,128)S(1)}) %tuple.205), branch_computations={%region_10.10_spmd, %region_11.11_spmd} | conditional | flops 2097188 | bytes 35652680 | solution.py:74
  515.9 19.3 %conditional.8 = (f32[1,16,4]{1,2,0:T(4,128)S(1)}) conditional(s32[]{:T(128)} %convert_element_type.36, () %tuple.203, (s32[4]{0:T(128)S(1)}, f32[16,512,128]{2,0,1:T(8,128)}, s32[16]{0:T(128)S(1)}, f32[4,512,128]{2,1,0:T(8,128)S(1)}) %tuple.205), branch_computations={%region_10.10_spmd, %region_11.11_spmd} | conditional | flops 2097188 | bytes 35652680 | solution.py:74
  548.3 19.3 %conditional.8 = (f32[1,16,4]{1,2,0:T(4,128)S(1)}) conditional(s32[]{:T(128)} %convert_element_type.36, () %tuple.203, (s32[4]{0:T(128)S(1)}, f32[16,512,128]{2,0,1:T(8,128)}, s32[16]{0:T(128)S(1)}, f32[4,512,128]{2,1,0:T(8,128)S(1)}) %tuple.205), branch_computations={%region_10.10_spmd, %region_11.11_spmd} | conditional | flops 2097188 | bytes 35652680 | solution.py:74
  580.7 19.3 %conditional.8 = (f32[1,16,4]{1,2,0:T(4,128)S(1)}) conditional(s32[]{:T(128)} %convert_element_type.36, () %tuple.203, (s32[4]{0:T(128)S(1)}, f32[16,512,128]{2,0,1:T(8,128)}, s32[16]{0:T(128)S(1)}, f32[4,512,128]{2,1,0:T(8,128)S(1)}) %tuple.205), branch_computations={%region_10.10_spmd, %region_11.11_spmd} | conditional | flops 2097188 | bytes 35652680 | solution.py:74
  613.2 19.3 %conditional.8 = (f32[1,16,4]{1,2,0:T(4,128)S(1)}) conditional(s32[]{:T(128)} %convert_element_type.36, () %tuple.203, (s32[4]{0:T(128)S(1)}, f32[16,512,128]{2,0,1:T(8,128)}, s32[16]{0:T(128)S(1)}, f32[4,512,128]{2,1,0:T(8,128)S(1)}) %tuple.205), branch_computations={%region_10.10_spmd, %region_11.11_spmd} | conditional | flops 2097188 | bytes 35652680 | solution.py:74
  645.6 19.3 %conditional.8 = (f32[1,16,4]{1,2,0:T(4,128)S(1)}) conditional(s32[]{:T(128)} %convert_element_type.36, () %tuple.203, (s32[4]{0:T(128)S(1)}, f32[16,512,128]{2,0,1:T(8,128)}, s32[16]{0:T(128)S(1)}, f32[4,512,128]{2,1,0:T(8,128)S(1)}) %tuple.205), branch_computations={%region_10.10_spmd, %region_11.11_spmd} | conditional | flops 2097188 | bytes 35652680 | solution.py:74
  678.0 19.3 %conditional.8 = (f32[1,16,4]{1,2,0:T(4,128)S(1)}) conditional(s32[]{:T(128)} %convert_element_type.36, () %tuple.203, (s32[4]{0:T(128)S(1)}, f32[16,512,128]{2,0,1:T(8,128)}, s32[16]{0:T(128)S(1)}, f32[4,512,128]{2,1,0:T(8,128)S(1)}) %tuple.205), branch_computations={%region_10.10_spmd, %region_11.11_spmd} | conditional | flops 2097188 | bytes 35652680 | solution.py:74
  710.4 19.3 %conditional.8 = (f32[1,16,4]{1,2,0:T(4,128)S(1)}) conditional(s32[]{:T(128)} %convert_element_type.36, () %tuple.203, (s32[4]{0:T(128)S(1)}, f32[16,512,128]{2,0,1:T(8,128)}, s32[16]{0:T(128)S(1)}, f32[4,512,128]{2,1,0:T(8,128)S(1)}) %tuple.205), branch_computations={%region_10.10_spmd, %region_11.11_spmd} | conditional | flops 2097188 | bytes 35652680 | solution.py:74
  732.3 45.0 %while.31 = (s32[]{:T(128)}, f32[512,512]{1,0:T(8,128)}, s32[16,2]{0,1:T(2,128)S(1)}, f32[16,128,512]{2,1,0:T(8,128)}, s32[]{:T(128)}) while((s32[]{:T(128)}, f32[512,512]{1,0:T(8,128)}, s32[16,2]{0,1:T(2,128)S(1)}, f32[16,128,512]{2,1,0:T(8,128)}, s32[]{:T(128)}) %tuple.221), condition=%wide.while_cond.3, body=%wide.while_body.3.sunk | while | flops 2 | bytes 525401 | solution.py:32
  777.3 8.8 fusion.16
  790.6 457.4 %while.29 = (s32[]{:T(128)}, f32[16,16,4]{1,2,0:T(4,128)S(1)}, pred[]{:T(512)}, s32[16]{0:T(128)S(1)}, s32[64]{0:T(128)S(1)}, /*index=5*/f32[512,512]{1,0:T(8,12...) while((s32[]{:T(128)}, f32[16,16,4]{1,2,0:T(4,128)S(1)}, ...), condition=%wide.region_16.17_spmd, body=%wide.region_13.16_spmd.sunk | while | flops 404750400 | bytes 38540844 | solution.py:139
  799.9 19.3 %conditional.9 = (f32[1,16,4]{1,2,0:T(4,128)S(1)}) conditional(s32[]{:T(128)} %convert_element_type.37, () %tuple.208, (s32[4]{0:T(128)S(1)}, f32[16,512,128]{2,0,1:T(8,128)}, s32[16]{0:T(128)S(1)}, f32[4,512,128]{2,1,0:T(8,128)S(1)}) %tuple.210), branch_computations={%region_14.14_spmd, %region_15.15_spmd} | conditional | flops 2097188 | bytes 35652680 | solution.py:74
  828.4 19.3 %conditional.9 = (f32[1,16,4]{1,2,0:T(4,128)S(1)}) conditional(s32[]{:T(128)} %convert_element_type.37, () %tuple.208, (s32[4]{0:T(128)S(1)}, f32[16,512,128]{2,0,1:T(8,128)}, s32[16]{0:T(128)S(1)}, f32[4,512,128]{2,1,0:T(8,128)S(1)}) %tuple.210), branch_computations={%region_14.14_spmd, %region_15.15_spmd} | conditional | flops 2097188 | bytes 35652680 | solution.py:74
  857.0 19.3 %conditional.9 = (f32[1,16,4]{1,2,0:T(4,128)S(1)}) conditional(s32[]{:T(128)} %convert_element_type.37, () %tuple.208, (s32[4]{0:T(128)S(1)}, f32[16,512,128]{2,0,1:T(8,128)}, s32[16]{0:T(128)S(1)}, f32[4,512,128]{2,1,0:T(8,128)S(1)}) %tuple.210), branch_computations={%region_14.14_spmd, %region_15.15_spmd} | conditional | flops 2097188 | bytes 35652680 | solution.py:74
  885.6 19.3 %conditional.9 = (f32[1,16,4]{1,2,0:T(4,128)S(1)}) conditional(s32[]{:T(128)} %convert_element_type.37, () %tuple.208, (s32[4]{0:T(128)S(1)}, f32[16,512,128]{2,0,1:T(8,128)}, s32[16]{0:T(128)S(1)}, f32[4,512,128]{2,1,0:T(8,128)S(1)}) %tuple.210), branch_computations={%region_14.14_spmd, %region_15.15_spmd} | conditional | flops 2097188 | bytes 35652680 | solution.py:74
  914.2 19.3 %conditional.9 = (f32[1,16,4]{1,2,0:T(4,128)S(1)}) conditional(s32[]{:T(128)} %convert_element_type.37, () %tuple.208, (s32[4]{0:T(128)S(1)}, f32[16,512,128]{2,0,1:T(8,128)}, s32[16]{0:T(128)S(1)}, f32[4,512,128]{2,1,0:T(8,128)S(1)}) %tuple.210), branch_computations={%region_14.14_spmd, %region_15.15_spmd} | conditional | flops 2097188 | bytes 35652680 | solution.py:74
  942.8 19.3 %conditional.9 = (f32[1,16,4]{1,2,0:T(4,128)S(1)}) conditional(s32[]{:T(128)} %convert_element_type.37, () %tuple.208, (s32[4]{0:T(128)S(1)}, f32[16,512,128]{2,0,1:T(8,128)}, s32[16]{0:T(128)S(1)}, f32[4,512,128]{2,1,0:T(8,128)S(1)}) %tuple.210), branch_computations={%region_14.14_spmd, %region_15.15_spmd} | conditional | flops 2097188 | bytes 35652680 | solution.py:74
  971.4 19.3 %conditional.9 = (f32[1,16,4]{1,2,0:T(4,128)S(1)}) conditional(s32[]{:T(128)} %convert_element_type.37, () %tuple.208, (s32[4]{0:T(128)S(1)}, f32[16,512,128]{2,0,1:T(8,128)}, s32[16]{0:T(128)S(1)}, f32[4,512,128]{2,1,0:T(8,128)S(1)}) %tuple.210), branch_computations={%region_14.14_spmd, %region_15.15_spmd} | conditional | flops 2097188 | bytes 35652680 | solution.py:74
  999.9 19.3 %conditional.9 = (f32[1,16,4]{1,2,0:T(4,128)S(1)}) conditional(s32[]{:T(128)} %convert_element_type.37, () %tuple.208, (s32[4]{0:T(128)S(1)}, f32[16,512,128]{2,0,1:T(8,128)}, s32[16]{0:T(128)S(1)}, f32[4,512,128]{2,1,0:T(8,128)S(1)}) %tuple.210), branch_computations={%region_14.14_spmd, %region_15.15_spmd} | conditional | flops 2097188 | bytes 35652680 | solution.py:74
  1028.5 19.3 %conditional.9 = (f32[1,16,4]{1,2,0:T(4,128)S(1)}) conditional(s32[]{:T(128)} %convert_element_type.37, () %tuple.208, (s32[4]{0:T(128)S(1)}, f32[16,512,128]{2,0,1:T(8,128)}, s32[16]{0:T(128)S(1)}, f32[4,512,128]{2,1,0:T(8,128)S(1)}) %tuple.210), branch_computations={%region_14.14_spmd, %region_15.15_spmd} | conditional | flops 2097188 | bytes 35652680 | solution.py:74
  1057.1 19.3 %conditional.9 = (f32[1,16,4]{1,2,0:T(4,128)S(1)}) conditional(s32[]{:T(128)} %convert_element_type.37, () %tuple.208, (s32[4]{0:T(128)S(1)}, f32[16,512,128]{2,0,1:T(8,128)}, s32[16]{0:T(128)S(1)}, f32[4,512,128]{2,1,0:T(8,128)S(1)}) %tuple.210), branch_computations={%region_14.14_spmd, %region_15.15_spmd} | conditional | flops 2097188 | bytes 35652680 | solution.py:74
  1085.7 19.3 %conditional.9 = (f32[1,16,4]{1,2,0:T(4,128)S(1)}) conditional(s32[]{:T(128)} %convert_element_type.37, () %tuple.208, (s32[4]{0:T(128)S(1)}, f32[16,512,128]{2,0,1:T(8,128)}, s32[16]{0:T(128)S(1)}, f32[4,512,128]{2,1,0:T(8,128)S(1)}) %tuple.210), branch_computations={%region_14.14_spmd, %region_15.15_spmd} | conditional | flops 2097188 | bytes 35652680 | solution.py:74
  1114.3 19.3 %conditional.9 = (f32[1,16,4]{1,2,0:T(4,128)S(1)}) conditional(s32[]{:T(128)} %convert_element_type.37, () %tuple.208, (s32[4]{0:T(128)S(1)}, f32[16,512,128]{2,0,1:T(8,128)}, s32[16]{0:T(128)S(1)}, f32[4,512,128]{2,1,0:T(8,128)S(1)}) %tuple.210), branch_computations={%region_14.14_spmd, %region_15.15_spmd} | conditional | flops 2097188 | bytes 35652680 | solution.py:74
  1142.9 19.3 %conditional.9 = (f32[1,16,4]{1,2,0:T(4,128)S(1)}) conditional(s32[]{:T(128)} %convert_element_type.37, () %tuple.208, (s32[4]{0:T(128)S(1)}, f32[16,512,128]{2,0,1:T(8,128)}, s32[16]{0:T(128)S(1)}, f32[4,512,128]{2,1,0:T(8,128)S(1)}) %tuple.210), branch_computations={%region_14.14_spmd, %region_15.15_spmd} | conditional | flops 2097188 | bytes 35652680 | solution.py:74
  1171.5 19.3 %conditional.9 = (f32[1,16,4]{1,2,0:T(4,128)S(1)}) conditional(s32[]{:T(128)} %convert_element_type.37, () %tuple.208, (s32[4]{0:T(128)S(1)}, f32[16,512,128]{2,0,1:T(8,128)}, s32[16]{0:T(128)S(1)}, f32[4,512,128]{2,1,0:T(8,128)S(1)}) %tuple.210), branch_computations={%region_14.14_spmd, %region_15.15_spmd} | conditional | flops 2097188 | bytes 35652680 | solution.py:74
  1200.0 19.3 %conditional.9 = (f32[1,16,4]{1,2,0:T(4,128)S(1)}) conditional(s32[]{:T(128)} %convert_element_type.37, () %tuple.208, (s32[4]{0:T(128)S(1)}, f32[16,512,128]{2,0,1:T(8,128)}, s32[16]{0:T(128)S(1)}, f32[4,512,128]{2,1,0:T(8,128)S(1)}) %tuple.210), branch_computations={%region_14.14_spmd, %region_15.15_spmd} | conditional | flops 2097188 | bytes 35652680 | solution.py:74
  1228.6 19.3 %conditional.9 = (f32[1,16,4]{1,2,0:T(4,128)S(1)}) conditional(s32[]{:T(128)} %convert_element_type.37, () %tuple.208, (s32[4]{0:T(128)S(1)}, f32[16,512,128]{2,0,1:T(8,128)}, s32[16]{0:T(128)S(1)}, f32[4,512,128]{2,1,0:T(8,128)S(1)}) %tuple.210), branch_computations={%region_14.14_spmd, %region_15.15_spmd} | conditional | flops 2097188 | bytes 35652680 | solution.py:74
  1248.0 89.4 %all-reduce.8 = f32[2,16,64]{2,1,0:T(8,128)S(1)} all-reduce(f32[2,16,64]{2,1,0:T(8,128)S(1)} %maximum_multiply_fusion), channel_id=2, replica_groups=mesh['bl'=8,'bp'=4] {'bl'}, use_global_device_ids=true, to_apply=%region_17.18.clone | all-reduce | flops 2048 | bytes 16384
  (1002 shorter events, 1217.0 us)
Async XLA Ops:
  6.5 51.2 %all-gather.2.cloned.1.call-start = ((), (), s32[]{:S(2)}) async-start(), calls=%async_computation | async-start | bytes 2621440 | tf_op jit(solution)/shard_map/all_gather | solution.py:100
  57.8 47.8 %collective-permute-start = (f32[1,2,512,512]{3,2,1,0:T(8,128)}, f32[1,2,512,512]{3,2,1,0:T(8,128)}, u32[]{:S(2)}, u32[]{:S(2)}) collective-permute-start(f32[1,2,512,512]{3,2,1,0:T(8,128)} %bitcast.114), channel_id=1, source_target_pairs={{0,28},{4,0},{8,4},{12,8},{16,12},{20,16},{24,20},{28,24},{1,29},{... | collective-permute-start | bytes 6291464 | tf_op jit(solution)/shard_map/ppermute | solution.py:18
  59.4 91.3 %collective-permute-start.1 = (f32[1,2,512,512]{3,2,1,0:T(8,128)}, f32[1,2,512,512]{3,2,1,0:T(8,128)S(1)}, u32[]{:S(2)}, u32[]{:S(2)}) collective-permute-start(f32[1,2,512,512]{3,2,1,0:T(8,128)} %bitcast.115), channel_id=1, source_target_pairs={{0,24},{4,28},{8,0},{12,4},{16,8},{20,12},{24,16},{28,20},{1,25},{... | collective-permute-start | bytes 6291464 | tf_op jit(solution)/shard_map/ppermute | solution.py:18
  60.1 90.8 %collective-permute-start.2 = (f32[1,2,512,512]{3,2,1,0:T(8,128)}, f32[1,2,512,512]{3,2,1,0:T(8,128)}, u32[]{:S(2)}, u32[]{:S(2)}) collective-permute-start(f32[1,2,512,512]{3,2,1,0:T(8,128)} %bitcast.116), channel_id=1, source_target_pairs={{0,20},{4,24},{8,28},{12,0},{16,4},{20,8},{24,12},{28,16},{1,21},{... | collective-permute-start | bytes 6291464 | tf_op jit(solution)/shard_map/ppermute | solution.py:18
  60.5 90.4 %collective-permute-start.3 = (f32[1,2,512,512]{3,2,1,0:T(8,128)}, f32[1,2,512,512]{3,2,1,0:T(8,128)}, u32[]{:S(2)}, u32[]{:S(2)}) collective-permute-start(f32[1,2,512,512]{3,2,1,0:T(8,128)} %bitcast.117), channel_id=1, source_target_pairs={{0,16},{4,20},{8,24},{12,28},{16,0},{20,4},{24,8},{28,12},{1,17},{... | collective-permute-start | bytes 6291464 | tf_op jit(solution)/shard_map/ppermute | solution.py:18
  67.4 4.9 copy-start
Sparse Core Ops, SparseCore 0:
  9.3 48.3 all-gather.1
where the time goes:
time: 1350 us; the launch traced here: 1340 us
  local copies, waits for them, and re-layouts  797 us (59%)
  other arithmetic  163 us (12%)
  waiting for transfers between devices  126 us (9%)
  matrix products  106 us (8%)
  blocking collectives  89.4 us (7%)
  loops' own time  44.6 us (3%)
  between operations  15.4 us (1%)
    gather x64, local copies, waits for them, and re-layouts, one_matrix(): lax.dynamic_slice_in_dim(matrix, row_start, window, 0)  309 us
    gather x480, local copies, waits for them, and re-layouts  285 us
    cond x32, other arithmetic  149 us
    cond x34, local copies, waits for them, and re-layouts  140 us
    dot_general x34, matrix products, project_turned(): jnp.einsum('apq,aqc->acp', kernels, window_rows, precision=highest, prefe...  106 us
    unnamed x1, blocking collectives  89.4 us
    ppermute x4, waiting for transfers between devices, passed_along(): return lax.ppermute(value, axis, pairs)  77.5 us
    all_gather x1, waiting for transfers between devices, body(): lax.all_gather(masked, 'bp', axis=1, tiled=True).reshape(full_shape)  48.5 us
  transfers between devices with their start and end apart: 5, of which 4 were waited for; matrix products, arithmetic and copies ran while one was open for 1% of the time, Pallas kernels for 0%

commit v1 on v0

v1 whole, which is shorter than its diff:
```python
from functools import partial

import jax
import jax.numpy as jnp
from jax import lax
from jax.experimental import pallas as pl
from jax.experimental.pallas import tpu as pltpu
from jax.sharding import PartitionSpec as P

WINDOW_LENGTH = 128
KINDS = 4
CHUNKS = 4
MESH = pl.DeviceIdType.MESH
NT = (((1,), (1,)), ((), ()))
NN = (((1,), (0,)), ((), ()))


def split(value):
    high = value.astype(jnp.bfloat16)
    return high, (value - high.astype(jnp.float32)).astype(jnp.bfloat16)


def dot(left, right, dims):
    return lax.dot_general(left, right, dims, preferred_element_type=jnp.float32)


def dot3(left, right, dims):
    return dot(left[0], right[0], dims) + (dot(left[0], right[1], dims) + dot(left[1], right[0], dims))


def exact(left, right, dims):
    return lax.dot_general(
        left, right, dims, precision=lax.Precision.HIGHEST, preferred_element_type=jnp.float32
    )


def column_of(row, length, offset):
    shape = (length, row.shape[1])
    spot = lax.broadcasted_iota(jnp.int32, shape, 0) + offset == lax.broadcasted_iota(jnp.int32, shape, 1)
    return jnp.sum(jnp.where(spot, row, 0.0), axis=1, keepdims=True)


def kernel(
    sizes, cov_ref, mask_ref, partner_ref, starts_ref, out_ref,
    raw, panel, near, far, sib_own, sib_near, sib_far, toep, toep_low, grown, other,
    inside, ramp, edge, edge_own, sums, tiles, landed, share, shares,
    load_sem, sib_sem, turn_sem, far_sem, near_sem, sfar_sem, snear_sem, fin_send, fin_recv, row_send, row_recv,
):
    groups, owners, rows, width, bands = sizes
    window = WINDOW_LENGTH
    me, level = lax.axis_index("bl"), lax.axis_index("bp")
    per_half = width // rows
    half, first = level // per_half, pl.multiple_of(level % per_half * rows, rows)
    pair, core = me // 2, me % 2
    pairs = groups // 2
    sibling = pair * 2 + 1 - core
    beside = (pair + 1 - 2 * (pair % 2)) * 2 + core
    behind = (pair + pairs - 2) % pairs * 2 + core
    level_other = level // per_half * per_half + (per_half - 1 - level % per_half)
    tile_rows = bands // groups
    band_share = bands // owners
    step = rows // CHUNKS

    load = pltpu.make_async_copy(
        cov_ref.at[0, :, pl.ds(pl.multiple_of(half * width, width), width)], raw, load_sem.at[0]
    )
    load.start()
    barrier = pltpu.get_barrier_semaphore()
    for d in range(1, groups):
        pl.semaphore_signal(barrier, inc=1, device_id=((me + d) % groups, level), device_id_type=MESH)
    for d in range(1, owners):
        pl.semaphore_signal(barrier, inc=1, device_id=(me, (level + d) % owners), device_id_type=MESH)

    marks = mask_ref[:, pl.ds(pl.multiple_of(half * width, width), width)].astype(jnp.float32)
    row_marks = column_of(marks, rows, first)
    load.wait()
    panel[pl.ds(first, rows), :] = raw[...] * row_marks * marks
    pl.semaphore_wait(barrier, groups + owners - 2)

    def remote(source, target, sems, index, device):
        return pltpu.make_async_remote_copy(
            src_ref=source, dst_ref=target, send_sem=sems.at[0, index], recv_sem=sems.at[1, index],
            device_id=device, device_id_type=MESH,
        )

    def own_at(q):
        return panel.at[pl.ds(pl.multiple_of(first + q * step, step), step)]

    def part(ref, q):
        return ref.at[pl.ds(q * step, step)]

    to_far = [remote(own_at(q), part(far, q), far_sem, q, (behind, level)) for q in range(CHUNKS)]
    near_direct = [remote(own_at(q), part(near, q), near_sem, q, (beside, level)) for q in range(CHUNKS)]
    near_relay = [remote(part(far, q), part(near, q), near_sem, q, (beside, level)) for q in range(CHUNKS)]
    far_on = [remote(part(far, q), part(sib_far, q), sfar_sem, q, (sibling, level)) for q in range(CHUNKS)]
    near_on = [remote(part(near, q), part(sib_near, q), snear_sem, q, (sibling, level)) for q in range(CHUNKS)]
    own_rows = panel.at[pl.ds(first, rows)]
    to_sibling = remote(own_rows, sib_own, sib_sem, 0, (sibling, level))
    to_turn = remote(own_rows, own_rows, turn_sem, 0, (me, level_other))
    other_first = pl.multiple_of(width - rows - first, rows)
    turn_in = panel.at[pl.ds(other_first, rows)]
    from_turn = remote(turn_in, turn_in, turn_sem, 0, (me, level_other))

    odd = pair % 2 == 1
    for q in range(CHUNKS):
        to_far[q].start()

        @pl.when(odd)
        def _():
            near_direct[q].start()

    to_turn.start()
    to_sibling.start()

    def relay(q):
        to_far[q].wait_recv()

        @pl.when(jnp.logical_not(odd))
        def _():
            near_relay[q].start()

        far_on[q].start()

    def forward(q):
        near_direct[q].wait_recv()
        near_on[q].start()

    def fill(kind, carry):
        far_apart = jnp.abs(
            lax.broadcasted_iota(jnp.int32, (width, width), 0) - lax.broadcasted_iota(jnp.int32, (width, width), 1)
        ).astype(jnp.float32)
        length = 1.0 + lax.convert_element_type(kind, jnp.float32)
        high, low = split(jnp.exp(-far_apart / length))
        toep[kind] = high
        toep_low[kind] = low
        return carry

    lax.fori_loop(0, KINDS, fill, 0)

    start_row = starts_ref[pl.ds(half, 1), :].astype(jnp.float32)
    start = column_of(start_row, bands, 0)
    band_ids = lax.broadcasted_iota(jnp.int32, (bands, 1), 0)
    inverse_length = 1.0 / (1.0 + (band_ids % KINDS).astype(jnp.float32))
    channel = lax.broadcasted_iota(jnp.int32, (bands, width), 1).astype(jnp.float32)
    ahead = channel - start
    past = ahead - (window - 1)
    within = jnp.logical_and(ahead >= 0.0, past <= 0.0)
    inside[...] = jnp.where(within, 1.0, 0.0)
    ramp[0:bands, :] = jnp.where(within, jnp.exp(-jnp.abs(ahead) * inverse_length), 0.0)
    ramp[bands:, :] = jnp.where(within, jnp.exp(-jnp.abs(past) * inverse_length), 0.0)
    edge[0:bands, :] = jnp.where(ahead < 0.0, jnp.exp(-jnp.abs(ahead) * inverse_length), 0.0)
    edge[bands:, :] = jnp.where(past > 0.0, jnp.exp(-jnp.abs(past) * inverse_length), 0.0)

    relay(0)
    relay(1)
    from_turn.wait_recv()
    ramps, edges = split(ramp[...]), split(edge[...])
    whole = split(panel[...])
    edge_own[...] = dot3(edges, whole, NN)

    def grow(kind, carry):
        mine = pl.ds(first, rows)
        grown[kind] = dot3((toep[kind, mine, :], toep_low[kind, mine, :]), whole, NN)
        sums[kind] = jnp.zeros((rows, bands), jnp.float32)
        return carry

    lax.fori_loop(0, KINDS // 2, grow, 0)
    relay(2)
    lax.fori_loop(KINDS // 2, KINDS, grow, 0)
    relay(3)
    across = dot3(split(edge_own[...]), ramps, NT)
    for q in range(CHUNKS):
        forward(q)
    to_sibling.wait_recv()
    for q in range(CHUNKS):
        far_on[q].wait_recv()
        near_on[q].wait_recv()

    def weight(baseline):
        total = jnp.float32(0.0)
        for slot in range(partner_ref.shape[1]):
            total = total + jnp.where(partner_ref[0, slot] == baseline, jnp.float32(1.0), jnp.float32(0.0))
        return total

    pair_near, pair_far = (pair + 1) % pairs * 2, (pair + 2) % pairs * 2
    summed = (
        sib_own[...] * weight(sibling)
        + near[...] * weight(pair_near + core)
        + far[...] * weight(pair_far + core)
        + sib_near[...] * weight(pair_near + 1 - core)
        + sib_far[...] * weight(pair_far + 1 - core)
    )
    partners = split(summed)
    mine = pl.ds(first, rows)
    ramp_mine = split(ramp[:, mine])
    leak = dot3(partners, edges, NT)
    inner = dot3(ramp_mine, split(leak), NN)
    cross = inner * across
    total = cross[0:bands, 0:bands] + cross[0:bands, bands:] + cross[bands:, 0:bands] + cross[bands:, bands:]

    other[...] = jnp.zeros((bands, 2 * bands), jnp.float32)

    def spread(kind, carry):
        turned = dot3(partners, (toep[kind], toep_low[kind]), NN)
        own_kind = (lax.broadcasted_iota(jnp.int32, (bands, 1), 0) % KINDS == kind).astype(jnp.float32)
        window_kind = (inside[...] * own_kind).astype(jnp.bfloat16)
        for m in range(KINDS):
            high, low = split(grown[m] * turned)
            sums[m] = sums[m] + (dot(high, window_kind, NT) + dot(low, window_kind, NT))
        high, low = split(dot3(ramp_mine, split(turned), NN) * edge_own[...])
        other[...] = other[...] + (dot(window_kind, high, NT) + dot(window_kind, low, NT))
        return carry

    lax.fori_loop(0, KINDS, spread, 0)
    inside_mine = inside[:, mine].astype(jnp.bfloat16)
    for m in range(KINDS):
        reach = leak * dot3(split(grown[m]), ramps, NT)
        high, low = split(sums[m] - reach[:, 0:bands] - reach[:, bands:])
        found = dot(inside_mine, high, NN) + dot(inside_mine, low, NN)
        total = total + jnp.where(band_ids % KINDS == m, found, 0.0)
    eye = (
        lax.broadcasted_iota(jnp.int32, (bands, bands), 0) == lax.broadcasted_iota(jnp.int32, (bands, bands), 1)
    ).astype(jnp.float32)
    side = other[...]
    flipped = exact(eye, total, NT) - side[:, 0:bands] - side[:, bands:]
    flipped = flipped * (1.0 / (4 * groups * window))

    for g in range(groups):
        tiles[g] = flipped[g * tile_rows:(g + 1) * tile_rows, :]
    landed[pl.ds(me, 1)] = tiles[pl.ds(me, 1)]
    outgoing = []
    for d in range(1, groups):
        peer = (me + d) % groups
        copy = pltpu.make_async_remote_copy(
            src_ref=tiles.at[peer], dst_ref=landed.at[me], send_sem=fin_send.at[peer], recv_sem=fin_recv.at[me],
            device_id=(peer, level), device_id_type=MESH,
        )
        copy.start()
        outgoing.append(copy)
    for d in range(1, groups):
        peer = (me + d) % groups
        pltpu.make_async_remote_copy(
            src_ref=tiles.at[peer], dst_ref=landed.at[peer], send_sem=fin_send.at[peer], recv_sem=fin_recv.at[peer],
            device_id=(peer, level), device_id_type=MESH,
        ).wait_recv()
    mine_sum = landed[0]
    for g in range(1, groups):
        mine_sum = mine_sum + landed[g]
    share[...] = mine_sum
    shares[pl.ds(level, 1)] = mine_sum[None]
    for d in range(1, owners):
        peer = (level + d) % owners
        copy = pltpu.make_async_remote_copy(
            src_ref=share, dst_ref=shares.at[level], send_sem=row_send.at[peer], recv_sem=row_recv.at[level],
            device_id=(me, peer), device_id_type=MESH,
        )
        copy.start()
        outgoing.append(copy)
    for d in range(1, owners):
        peer = (level + d) % owners
        pltpu.make_async_remote_copy(
            src_ref=share, dst_ref=shares.at[peer], send_sem=row_send.at[peer], recv_sem=row_recv.at[peer],
            device_id=(me, peer), device_id_type=MESH,
        ).wait_recv()
    pick = (
        lax.broadcasted_iota(jnp.int32, (band_share, bands), 0) + level * band_share
        == lax.broadcasted_iota(jnp.int32, (band_share, bands), 1)
    ).astype(jnp.float32)
    for h in range(2):
        tile = shares[h * per_half]
        for k in range(1, per_half):
            tile = tile + shares[h * per_half + k]
        out_ref[h] = exact(pick, tile, NT)

    for copy in outgoing:
        copy.wait_send()
    for q in range(CHUNKS):
        to_far[q].wait_send()
        near_direct[q].wait_send()
        far_on[q].wait_send()
        near_on[q].wait_send()
    to_sibling.wait_send()
    to_turn.wait_send()


def solution(mesh):
    groups, owners = mesh.shape["bl"], mesh.shape["bp"]

    def body(inverse_cov, channel_keep_mask, partner_ids, band_starts):
        count, rows, channels = inverse_cov.shape
        width, bands = channels // 2, band_starts.shape[1]
        assert count == 1 and groups % 4 == 0 and width == 2 * rows
        f32, bf16 = jnp.float32, jnp.bfloat16
        block = pltpu.VMEM((rows, width), f32)
        tile_rows = bands // groups
        dma = pltpu.SemaphoreType.DMA
        vmem = pl.BlockSpec(memory_space=pltpu.VMEM)
        return pl.pallas_call(
            partial(kernel, (groups, owners, rows, width, bands)),
            name="fisher",
            out_shape=jax.ShapeDtypeStruct((2, bands // owners, tile_rows), f32),
            in_specs=[pl.BlockSpec(memory_space=pl.ANY), vmem, pl.BlockSpec(memory_space=pltpu.SMEM), vmem],
            out_specs=vmem,
            scratch_shapes=[
                block,
                pltpu.VMEM((width, width), f32),
                block, block, block, block, block,
                pltpu.VMEM((KINDS, width, width), bf16),
                pltpu.VMEM((KINDS, width, width), bf16),
                pltpu.VMEM((KINDS, rows, width), f32),
                pltpu.VMEM((bands, 2 * bands), f32),
                pltpu.VMEM((bands, width), f32),
                pltpu.VMEM((2 * bands, width), f32),
                pltpu.VMEM((2 * bands, width), f32),
                pltpu.VMEM((2 * bands, width), f32),
                pltpu.VMEM((KINDS, rows, bands), f32),
                pltpu.VMEM((groups, tile_rows, bands), f32),
                pltpu.VMEM((groups, tile_rows, bands), f32),
                pltpu.VMEM((tile_rows, bands), f32),
                pltpu.VMEM((owners, tile_rows, bands), f32),
                dma((1,)), dma((2, 1)), dma((2, 1)),
                dma((2, CHUNKS)), dma((2, CHUNKS)), dma((2, CHUNKS)), dma((2, CHUNKS)),
                dma((groups,)), dma((groups,)), dma((owners,)), dma((owners,)),
            ],
            compiler_params=pltpu.CompilerParams(
                collective_id=0, has_side_effects=True, vmem_limit_bytes=48 * 1024 * 1024
            ),
        )(inverse_cov, channel_keep_mask, partner_ids, band_starts)

    placed = (P("bl", "bp", None), P("bl", None), P("bl", None), P())
    return jax.shard_map(body, mesh=mesh, in_specs=placed, out_specs=P(None, "bp", "bl"), check_vma=False)
```

time: 1350 us -> 49.3 us (0.04)
  local copies, waits for them, and re-layouts: 797 us -> 3.91 us
  other arithmetic: 163 us -> 0 us
  waiting for transfers between devices: 126 us -> 0 us
  matrix products: 106 us -> 0 us
  blocking collectives: 89.4 us -> 0 us
  Pallas kernels: 0 us -> 45.2 us
  loops' own time: 44.6 us -> 0 us
  between operations: 15.4 us -> 0.01 us
    gather x544 -> x0, local copies, waits for them, and re-layouts: 594 us -> none  [the longest x64 309 us: one_matrix(): lax.dynamic_slice_in_dim(matrix, row_start, window, 0)]
    cond x32 -> x0, other arithmetic: 149 us -> none
    cond x34 -> x0, local copies, waits for them, and re-layouts: 140 us -> none
    dot_general x34 -> x0, matrix products: 106 us -> none  [project_turned(): jnp.einsum('apq,aqc->acp', kernels, window_rows, precision=highest, prefe...]
    unnamed x1 -> x0, blocking collectives: 89.4 us -> none
    ppermute x4 -> x0, waiting for transfers between devices: 77.5 us -> none  [passed_along(): return lax.ppermute(value, axis, pairs)]
    all_gather x1 -> x0, waiting for transfers between devices: 48.5 us -> none  [body(): lax.all_gather(masked, 'bp', axis=1, tiled=True).reshape(full_shape)]
    pallas_call x0 -> x1, Pallas kernels: none -> 45.2 us  [body(): pl.pallas_call(partial(kernel, (groups, owners, rows, width, bands)), nam...]
  transfers between devices with their start and end apart: 5 -> 0, of which waited for: 4 -> 0; matrix products, arithmetic and copies ran while one was open for 1% -> 0% of each run, Pallas kernels for 0% -> 0%
where the time goes in v1:
time: 49.3 us; the launch traced here: 49.1 us
  Pallas kernels  45.2 us (92%)
  local copies, waits for them, and re-layouts  3.91 us (8%)
    pallas_call x1, Pallas kernels, body(): pl.pallas_call(partial(kernel, (groups, owners, rows, width, bands)), nam...  45.2 us
    unnamed x8, local copies, waits for them, and re-layouts  3.24 us

profile of v1, /device:TPU:0, one launch (start us, length us, event | category | flops | bytes accessed | tf_op | source)
XLA Modules:
  0.0 49.1 jit_solution(2598471299078030747)
XLA Ops:
  0.0 0.0 copy-start
  0.0 1.2 %copy-done = f32[1,256,1024]{2,1,0:T(8,128)S(1)} copy-done((f32[1,256,1024]{2,1,0:T(8,128)S(1)}, f32[1,256,1024]{2,1,0:T(8,128)}, u32[]{:S(2)}) %copy-start) | copy-done | bytes 1048600
  1.2 0.0 copy-start.1
  1.2 0.7 %copy-done.1 = s32[1,1024]{1,0:T(1,128)S(1)} copy-done((s32[1,1024]{1,0:T(1,128)S(1)}, s32[1,1024]{1,0:T(1,128)}, u32[]{:S(2)}) %copy-start.1) | copy-done | bytes 4120
  1.9 0.0 copy-start.2
  1.9 0.7 %copy-done.2 = s32[2,64]{1,0:T(2,128)S(1)} copy-done((s32[2,64]{1,0:T(2,128)S(1)}, s32[2,64]{1,0:T(2,128)}, u32[]{:S(2)}) %copy-start.2) | copy-done | bytes 536
  2.6 0.0 copy-start.3
  2.6 0.7 %copy-done.3 = s32[1,2]{1,0:T(1,128)S(1)} copy-done((s32[1,2]{1,0:T(1,128)S(1)}, s32[1,2]{1,0:T(1,128)}, u32[]{:S(2)}) %copy-start.3) | copy-done | bytes 32
  3.2 45.2 %fisher.1 = f32[2,16,8]{2,1,0:T(8,128)S(1)} custom-call(f32[1,256,1024]{2,1,0:T(8,128)S(1)} %copy-done, s32[1,1024]{1,0:T(1,128)S(1)} %copy-done.1, s32[1,2]{1,0:T(1,128)S(1)} %copy-done.3, s32[2,64]{1,0:T(2,128)S(1)} %copy-done.2), custom_call_target="tpu_custom_call" | custom-call | tf_op jit(solution)/shard_map/fisher/pallas_call | solution.py:298
  48.4 0.7 %copy.5 = f32[2,16,8]{1,2,0:T(8,128)} copy(f32[2,16,8]{2,1,0:T(8,128)S(1)} %fisher.1) | data formatting | bytes 2048 | tf_op jit(solution)/shard_map/fisher/pallas_call | solution.py:298
Async XLA Ops:
  0.0 1.2 %copy-start = (f32[1,256,1024]{2,1,0:T(8,128)S(1)}, f32[1,256,1024]{2,1,0:T(8,128)}, u32[]{:S(2)}) copy-start(f32[1,256,1024]{2,1,0:T(8,128)} %cov_ref.1) | copy-start | bytes 3145732
  1.2 0.7 %copy-start.1 = (s32[1,1024]{1,0:T(1,128)S(1)}, s32[1,1024]{1,0:T(1,128)}, u32[]{:S(2)}) copy-start(s32[1,1024]{1,0:T(1,128)} %mask_ref.1) | copy-start | bytes 12292
  1.9 0.7 %copy-start.2 = (s32[2,64]{1,0:T(2,128)S(1)}, s32[2,64]{1,0:T(2,128)}, u32[]{:S(2)}) copy-start(s32[2,64]{1,0:T(2,128)} %starts_ref.1) | copy-start | bytes 1540
  2.6 0.7 %copy-start.3 = (s32[1,2]{1,0:T(1,128)S(1)}, s32[1,2]{1,0:T(1,128)}, u32[]{:S(2)}) copy-start(s32[1,2]{1,0:T(1,128)} %partner_ref.1) | copy-start | bytes 28

commit v2 on v1

v2 whole, which is shorter than its diff:
```python
from functools import partial

import jax
import jax.numpy as jnp
from jax import lax
from jax.experimental import pallas as pl
from jax.experimental.pallas import tpu as pltpu
from jax.sharding import PartitionSpec as P

WINDOW_LENGTH = 128
KINDS = 4
CHUNKS = 8
MESH = pl.DeviceIdType.MESH
NT = (((1,), (1,)), ((), ()))
NN = (((1,), (0,)), ((), ()))


def split(value):
    high = value.astype(jnp.bfloat16)
    return high, (value - high.astype(jnp.float32)).astype(jnp.bfloat16)


def dot(left, right, dims):
    return lax.dot_general(left, right, dims, preferred_element_type=jnp.float32)


def dot3(left, right, dims):
    return dot(left[0], right[0], dims) + (dot(left[0], right[1], dims) + dot(left[1], right[0], dims))


def exact(left, right, dims):
    return lax.dot_general(
        left, right, dims, precision=lax.Precision.HIGHEST, preferred_element_type=jnp.float32
    )


def column_of(row, length, offset):
    shape = (length, row.shape[1])
    spot = lax.broadcasted_iota(jnp.int32, shape, 0) + offset == lax.broadcasted_iota(jnp.int32, shape, 1)
    return jnp.sum(jnp.where(spot, row, 0.0), axis=1, keepdims=True)


def kernel(
    sizes, cov_ref, mask_ref, partner_ref, starts_ref, out_ref,
    raw, masks, partner_row, starts, panel, near, far, sib_own, sib_near, sib_far, toep, toep_low, grown, felt,
    windows, ramp, edge, edge_own, crossed, tiles, landed, share, shares,
    load_sem, sib_sem, turn_sem, far_sem, near_sem, sfar_sem, snear_sem, fin_send, fin_recv, row_send, row_recv,
):
    groups, owners, rows, width, bands = sizes
    window = WINDOW_LENGTH
    me, level = lax.axis_index("bl"), lax.axis_index("bp")
    per_half = width // rows
    half, first = level // per_half, pl.multiple_of(level % per_half * rows, rows)
    pair, core = me // 2, me % 2
    pairs = groups // 2
    sibling = pair * 2 + 1 - core
    beside = (pair + 1 - 2 * (pair % 2)) * 2 + core
    behind = (pair + pairs - 2) % pairs * 2 + core
    level_other = level // per_half * per_half + (per_half - 1 - level % per_half)
    tile_rows = bands // groups
    band_share = bands // owners
    step = rows // CHUNKS

    half_columns = pl.ds(pl.multiple_of(half * width, width), width)
    loads = [
        pltpu.make_async_copy(source, target, load_sem.at[index])
        for index, (source, target) in enumerate([
            (cov_ref.at[0, :, half_columns], raw),
            (mask_ref, masks),
            (starts_ref, starts),
            (partner_ref, partner_row),
        ])
    ]
    for load in loads:
        load.start()
    barrier = pltpu.get_barrier_semaphore()
    for d in range(1, groups):
        pl.semaphore_signal(barrier, inc=1, device_id=((me + d) % groups, level), device_id_type=MESH)
    for d in range(1, owners):
        pl.semaphore_signal(barrier, inc=1, device_id=(me, (level + d) % owners), device_id_type=MESH)
    for load in loads:
        load.wait()

    marks = masks[:, half_columns].astype(jnp.float32)
    row_marks = column_of(marks, rows, first)
    panel[pl.ds(first, rows), :] = raw[...] * row_marks * marks
    pl.semaphore_wait(barrier, groups + owners - 2)

    def remote(source, target, sems, index, device):
        return pltpu.make_async_remote_copy(
            src_ref=source, dst_ref=target, send_sem=sems.at[0, index], recv_sem=sems.at[1, index],
            device_id=device, device_id_type=MESH,
        )

    def own_at(q):
        return panel.at[pl.ds(pl.multiple_of(first + q * step, step), step)]

    def part(ref, q):
        return ref.at[pl.ds(q * step, step)]

    to_far = [remote(own_at(q), part(far, q), far_sem, q, (behind, level)) for q in range(CHUNKS)]
    near_direct = [remote(own_at(q), part(near, q), near_sem, q, (beside, level)) for q in range(CHUNKS)]
    near_relay = [remote(part(far, q), part(near, q), near_sem, q, (beside, level)) for q in range(CHUNKS)]
    far_on = [remote(part(far, q), part(sib_far, q), sfar_sem, q, (sibling, level)) for q in range(CHUNKS)]
    near_on = [remote(part(near, q), part(sib_near, q), snear_sem, q, (sibling, level)) for q in range(CHUNKS)]
    own_rows = panel.at[pl.ds(first, rows)]
    to_sibling = remote(own_rows, sib_own, sib_sem, 0, (sibling, level))
    to_turn = remote(own_rows, own_rows, turn_sem, 0, (me, level_other))
    turn_in = panel.at[pl.ds(pl.multiple_of(width - rows - first, rows), rows)]
    from_turn = remote(turn_in, turn_in, turn_sem, 0, (me, level_other))

    odd = pair % 2 == 1
    for q in range(CHUNKS):
        to_far[q].start()

        @pl.when(odd)
        def _():
            near_direct[q].start()

    to_turn.start()
    to_sibling.start()

    def relay(q):
        to_far[q].wait_recv()

        @pl.when(jnp.logical_not(odd))
        def _():
            near_relay[q].start()

        far_on[q].start()

    def forward(q):
        near_direct[q].wait_recv()
        near_on[q].start()

    far_apart = jnp.abs(
        lax.broadcasted_iota(jnp.int32, (rows, rows), 0) - lax.broadcasted_iota(jnp.int32, (rows, rows), 1)
    ).astype(jnp.float32)
    for kind in range(KINDS):
        toep[kind], toep_low[kind] = split(jnp.exp(far_apart * (-1.0 / (1 + kind))))
    toeplitz = [(toep[kind], toep_low[kind]) for kind in range(KINDS)]

    start = column_of(starts[pl.ds(half, 1), :].astype(jnp.float32), bands, 0)
    band_ids = lax.broadcasted_iota(jnp.int32, (bands, 1), 0)
    inverse_length = 1.0 / (1.0 + (band_ids % KINDS).astype(jnp.float32))
    channel = lax.broadcasted_iota(jnp.int32, (bands, width), 1).astype(jnp.float32)
    ahead = channel - start
    past = ahead - (window - 1)
    within = jnp.logical_and(ahead >= 0.0, past <= 0.0)
    for kind in range(KINDS):
        windows[kind] = jnp.where(jnp.logical_and(within, band_ids % KINDS == kind), 1.0, 0.0).astype(jnp.bfloat16)
    windows[KINDS] = jnp.where(within, 1.0, 0.0).astype(jnp.bfloat16)
    rise, fall = jnp.exp(-jnp.abs(ahead) * inverse_length), jnp.exp(-jnp.abs(past) * inverse_length)
    ramp[0:bands, :] = jnp.where(within, rise, 0.0)
    ramp[bands:, :] = jnp.where(within, fall, 0.0)
    edge[0:bands, :] = jnp.where(ahead < 0.0, rise, 0.0)
    edge[bands:2 * bands, :] = jnp.where(past > 0.0, fall, 0.0)
    carry_ids = lax.broadcasted_iota(jnp.int32, (2 * KINDS, 1), 0)
    carry_length = 1.0 / (1.0 + (carry_ids % KINDS).astype(jnp.float32))
    carry_channel = lax.broadcasted_iota(jnp.int32, (2 * KINDS, width), 1).astype(jnp.float32) - rows
    upper = carry_ids < KINDS
    carry_gap = jnp.where(upper, carry_channel, -1.0 - carry_channel)
    edge[2 * bands:, :] = jnp.where(carry_gap >= 0.0, jnp.exp(-jnp.abs(carry_gap) * carry_length), 0.0)

    mine = pl.ds(first, rows)
    own_split = split(panel[mine, :])
    relay(0)
    for kind in range(KINDS):
        grown[kind] = dot3(toeplitz[kind], own_split, NN)
    relay(1)
    relay(2)
    from_turn.wait_recv()
    edges = split(edge[...])
    edge_own[...] = dot3(edges, split(panel[...]), NN)
    relay(3)
    ramps = split(ramp[...])
    place = lax.broadcasted_iota(jnp.int32, (rows, 1), 0)
    reach_in = jnp.where(first == 0, rows - place, place + 1).astype(jnp.float32)
    for kind in range(KINDS):
        carry = jnp.where(
            first == 0,
            edge_own[2 * bands + kind:2 * bands + kind + 1, :],
            edge_own[2 * bands + KINDS + kind:2 * bands + KINDS + kind + 1, :],
        )
        grown[kind] = grown[kind] + jnp.exp(reach_in * (-1.0 / (1 + kind))) * carry
        felt[kind] = dot3(split(grown[kind]), ramps, NT)
        if kind == 1:
            relay(4)
    own_edges = edge_own[0:2 * bands, :]
    across = dot3(split(own_edges), ramps, NT)
    relay(5)
    middle = CHUNKS // 2
    for q in range(middle):
        forward(q)
    to_sibling.wait_recv()

    def weight(baseline):
        return jnp.sum(jnp.where(partner_row[...] == baseline, 1.0, 0.0), axis=1, keepdims=True)

    pair_near, pair_far = (pair + 1) % pairs * 2, (pair + 2) % pairs * 2
    weights = [
        (sib_own, weight(sibling)), (near, weight(pair_near + core)), (far, weight(pair_far + core)),
        (sib_near, weight(pair_near + 1 - core)), (sib_far, weight(pair_far + 1 - core)),
    ]
    lane = lax.broadcasted_iota(jnp.int32, (1, rows), 1)

    def join(part_index, total, chores):
        span = rows // 2
        low_row = part_index * span
        for q in range(part_index * middle, (part_index + 1) * middle):
            far_on[q].wait_recv()
            near_on[q].wait_recv()
        here = slice(low_row, low_row + span)
        summed = sum(ref[here, :] * factor for ref, factor in weights)
        partners = split(summed)
        columns = pl.ds(pl.multiple_of(first + low_row, span), span)
        ramp_here = split(ramp[:, columns])
        leak = dot3(partners, edges, NT)
        leak_bands = leak[:, 0:2 * bands]
        inner = dot3(ramp_here, split(leak_bands), NN)
        sums = jnp.zeros((KINDS * span, bands), jnp.float32)
        for kind in range(KINDS):
            if kind < len(chores):
                chores[kind]()
            left = dot3((partners[0][:, 0:rows], partners[1][:, 0:rows]), toeplitz[kind], NN)
            left = left + leak[:, 2 * bands + kind:2 * bands + kind + 1] * jnp.exp(
                (rows - lane).astype(jnp.float32) * (-1.0 / (1 + kind)))
            right = dot3((partners[0][:, rows:], partners[1][:, rows:]), toeplitz[kind], NN)
            right = right + leak[:, 2 * bands + KINDS + kind:2 * bands + KINDS + kind + 1] * jnp.exp(
                (lane + 1).astype(jnp.float32) * (-1.0 / (1 + kind)))
            turned = jnp.concatenate([left, right], axis=1)
            pieces = [split(grown[m, here, :] * turned) for m in range(KINDS)]
            stacked = jnp.concatenate([p[0] for p in pieces] + [p[1] for p in pieces], axis=0)
            boxed = dot(stacked, windows[kind], NT)
            sums = sums + (boxed[0:KINDS * span] + boxed[KINDS * span:])
            found = dot3(ramp_here, split(turned), NN)
            crossed[kind] = found if part_index == 0 else crossed[kind] + found
        inside_here = windows[KINDS, :, columns]
        for m in range(KINDS):
            reach = leak_bands * felt[m, here, :]
            high, low = split(sums[m * span:(m + 1) * span] - reach[:, 0:bands] - reach[:, bands:])
            total = total + jnp.where(
                band_ids % KINDS == m, dot(inside_here, high, NN) + dot(inside_here, low, NN), 0.0)
        return inner, total

    inner_0, total = join(0, jnp.zeros((bands, bands), jnp.float32), [
        lambda: relay(6), lambda: relay(7), lambda: forward(4), lambda: forward(5)])
    for q in range(6, CHUNKS):
        forward(q)
    inner_1, total = join(1, total, [])
    cross = (inner_0 + inner_1) * across
    total = total + cross[0:bands, 0:bands] + cross[0:bands, bands:] + cross[bands:, 0:bands] + cross[bands:, bands:]
    side = jnp.zeros((bands, 2 * bands), jnp.float32)
    for kind in range(KINDS):
        high, low = split(crossed[kind] * own_edges)
        side = side + (dot(windows[kind], high, NT) + dot(windows[kind], low, NT))
    eye = (
        lax.broadcasted_iota(jnp.int32, (bands, bands), 0) == lax.broadcasted_iota(jnp.int32, (bands, bands), 1)
    ).astype(jnp.float32)
    flipped = exact(eye, total, NT) - side[:, 0:bands] - side[:, bands:]
    flipped = flipped * (1.0 / (4 * groups * window))

    for g in range(groups):
        tiles[g] = flipped[g * tile_rows:(g + 1) * tile_rows, :]
    landed[pl.ds(me, 1)] = tiles[pl.ds(me, 1)]
    outgoing = []
    for d in range(1, groups):
        peer = (me + d) % groups
        copy = pltpu.make_async_remote_copy(
            src_ref=tiles.at[peer], dst_ref=landed.at[me], send_sem=fin_send.at[peer], recv_sem=fin_recv.at[me],
            device_id=(peer, level), device_id_type=MESH,
        )
        copy.start()
        outgoing.append(copy)
    for d in range(1, groups):
        peer = (me + d) % groups
        pltpu.make_async_remote_copy(
            src_ref=tiles.at[peer], dst_ref=landed.at[peer], send_sem=fin_send.at[peer], recv_sem=fin_recv.at[peer],
            device_id=(peer, level), device_id_type=MESH,
        ).wait_recv()
    mine_sum = landed[0]
    for g in range(1, groups):
        mine_sum = mine_sum + landed[g]
    share[...] = mine_sum
    shares[pl.ds(level, 1)] = mine_sum[None]
    for d in range(1, owners):
        peer = (level + d) % owners
        copy = pltpu.make_async_remote_copy(
            src_ref=share, dst_ref=shares.at[level], send_sem=row_send.at[peer], recv_sem=row_recv.at[level],
            device_id=(me, peer), device_id_type=MESH,
        )
        copy.start()
        outgoing.append(copy)
    for d in range(1, owners):
        peer = (level + d) % owners
        pltpu.make_async_remote_copy(
            src_ref=share, dst_ref=shares.at[peer], send_sem=row_send.at[peer], recv_sem=row_recv.at[peer],
            device_id=(me, peer), device_id_type=MESH,
        ).wait_recv()
    pick = (
        lax.broadcasted_iota(jnp.int32, (band_share, bands), 0) + level * band_share
        == lax.broadcasted_iota(jnp.int32, (band_share, bands), 1)
    ).astype(jnp.float32)
    for h in range(2):
        tile = shares[h * per_half]
        for k in range(1, per_half):
            tile = tile + shares[h * per_half + k]
        out_ref[h] = exact(tile, pick, NT)

    for copy in outgoing:
        copy.wait_send()
    for q in range(CHUNKS):
        to_far[q].wait_send()
        near_direct[q].wait_send()
        far_on[q].wait_send()
        near_on[q].wait_send()
    to_sibling.wait_send()
    to_turn.wait_send()


def solution(mesh):
    groups, owners = mesh.shape["bl"], mesh.shape["bp"]

    def body(inverse_cov, channel_keep_mask, partner_ids, band_starts):
        count, rows, channels = inverse_cov.shape
        width, bands = channels // 2, band_starts.shape[1]
        assert count == 1 and groups % 4 == 0 and width == 2 * rows
        f32, bf16 = jnp.float32, jnp.bfloat16
        block = pltpu.VMEM((rows, width), f32)
        tile_rows = bands // groups
        dma = pltpu.SemaphoreType.DMA
        vmem = pl.BlockSpec(memory_space=pltpu.VMEM)
        found = pl.pallas_call(
            partial(kernel, (groups, owners, rows, width, bands)),
            name="fisher",
            out_shape=jax.ShapeDtypeStruct((2, tile_rows, bands // owners), f32),
            in_specs=[pl.BlockSpec(memory_space=pltpu.HBM)] * 4,
            out_specs=vmem,
            scratch_shapes=[
                block,
                pltpu.VMEM(channel_keep_mask.shape, jnp.int32),
                pltpu.VMEM(partner_ids.shape, jnp.int32),
                pltpu.VMEM(band_starts.shape, jnp.int32),
                pltpu.VMEM((width, width), f32),
                block, block, block, block, block,
                pltpu.VMEM((KINDS, rows, rows), bf16),
                pltpu.VMEM((KINDS, rows, rows), bf16),
                pltpu.VMEM((KINDS, rows, width), f32),
                pltpu.VMEM((KINDS, rows, 2 * bands), f32),
                pltpu.VMEM((KINDS + 1, bands, width), bf16),
                pltpu.VMEM((2 * bands, width), f32),
                pltpu.VMEM((2 * bands + 2 * KINDS, width), f32),
                pltpu.VMEM((2 * bands + 2 * KINDS, width), f32),
                pltpu.VMEM((KINDS, 2 * bands, width), f32),
                pltpu.VMEM((groups, tile_rows, bands), f32),
                pltpu.VMEM((groups, tile_rows, bands), f32),
                pltpu.VMEM((tile_rows, bands), f32),
                pltpu.VMEM((owners, tile_rows, bands), f32),
                dma((4,)), dma((2, 1)), dma((2, 1)),
                dma((2, CHUNKS)), dma((2, CHUNKS)), dma((2, CHUNKS)), dma((2, CHUNKS)),
                dma((groups,)), dma((groups,)), dma((owners,)), dma((owners,)),
            ],
            compiler_params=pltpu.CompilerParams(
                collective_id=0, has_side_effects=True, vmem_limit_bytes=67043328
            ),
        )(inverse_cov, channel_keep_mask, partner_ids, band_starts)
        return jnp.swapaxes(found, 1, 2)

    placed = (P("bl", "bp", None), P("bl", None), P("bl", None), P())
    return jax.shard_map(body, mesh=mesh, in_specs=placed, out_specs=P(None, "bp", "bl"), check_vma=False)
```

time: 49.3 us -> 42.5 us (0.86)
  Pallas kernels: 45.2 us -> 41 us
  local copies, waits for them, and re-layouts: 3.91 us -> 1.3 us
    pallas_call x1, Pallas kernels: 45.2 us -> 41 us  [body(): pl.pallas_call(partial(kernel, (groups, owners, rows, width, bands)), nam...]
    unnamed x8 -> x1, local copies, waits for them, and re-layouts: 3.24 us -> 1.3 us
    pallas_call x1 -> x0, local copies, waits for them, and re-layouts: 0.67 us -> none  [body(): pl.pallas_call(partial(kernel, (groups, owners, rows, width, bands)), nam...]
where the time goes in v2:
time: 42.5 us; the launch traced here: 42.3 us
  Pallas kernels  41 us (96%)
  local copies, waits for them, and re-layouts  1.3 us (3%)
    pallas_call x1, Pallas kernels, body(): pl.pallas_call(partial(kernel, (groups, owners, rows, width, bands)), nam...  41 us
    unnamed x1, local copies, waits for them, and re-layouts  1.3 us

profile of v2, /device:TPU:0, one launch (start us, length us, event | category | flops | bytes accessed | tf_op | source)
XLA Modules:
  0.0 42.3 jit_solution(13576878791775978908)
XLA Ops:
  0.0 41.0 %fisher.1 = f32[2,8,16]{2,1,0:T(8,128)} custom-call(f32[1,256,1024]{2,1,0:T(8,128)} %cov_ref.1, s32[1,1024]{1,0:T(1,128)} %mask_ref.1, s32[1,2]{1,0:T(1,128)} %partner_ref.1, s32[2,64]{1,0:T(2,128)} %starts_ref.1), custom_call_target="tpu_custom_call" | custom-call | tf_op jit(solution)/shard_map/fisher/pallas_call | solution.py:333
  41.0 1.3 %copy.6 = f32[2,16,8]{1,2,0:T(8,128)} copy(f32[2,16,8]{1,2,0:T(8,128)} %bitcast.1) | data formatting | bytes 2048

commit v3 on v2

--- a/solution.py
+++ b/solution.py
@@ -42,7 +42,7 @@
 
 def kernel(
     sizes, cov_ref, mask_ref, partner_ref, starts_ref, out_ref,
-    raw, masks, partner_row, starts, panel, near, far, sib_own, sib_near, sib_far, toep, toep_low, grown, felt,
+    raw, masks, partner_row, starts, panel, turn, near, far, sib_own, sib_near, sib_far, toep, toep_low, grown, felt,
     windows, ramp, edge, edge_own, crossed, tiles, landed, share, shares,
     load_sem, sib_sem, turn_sem, far_sem, near_sem, sfar_sem, snear_sem, fin_send, fin_recv, row_send, row_recv,
 ):
@@ -83,7 +83,7 @@
 
     marks = masks[:, half_columns].astype(jnp.float32)
     row_marks = column_of(marks, rows, first)
-    panel[pl.ds(first, rows), :] = raw[...] * row_marks * marks
+    panel[...] = raw[...] * row_marks * marks
     pl.semaphore_wait(barrier, groups + owners - 2)
 
     def remote(source, target, sems, index, device):
@@ -93,7 +93,7 @@
         )
 
     def own_at(q):
-        return panel.at[pl.ds(pl.multiple_of(first + q * step, step), step)]
+        return panel.at[pl.ds(q * step, step)]
 
     def part(ref, q):
         return ref.at[pl.ds(q * step, step)]
@@ -103,11 +103,10 @@
     near_relay = [remote(part(far, q), part(near, q), near_sem, q, (beside, level)) for q in range(CHUNKS)]
     far_on = [remote(part(far, q), part(sib_far, q), sfar_sem, q, (sibling, level)) for q in range(CHUNKS)]
     near_on = [remote(part(near, q), part(sib_near, q), snear_sem, q, (sibling, level)) for q in range(CHUNKS)]
-    own_rows = panel.at[pl.ds(first, rows)]
-    to_sibling = remote(own_rows, sib_own, sib_sem, 0, (sibling, level))
-    to_turn = remote(own_rows, own_rows, turn_sem, 0, (me, level_other))
-    turn_in = panel.at[pl.ds(pl.multiple_of(width - rows - first, rows), rows)]
-    from_turn = remote(turn_in, turn_in, turn_sem, 0, (me, level_other))
+    mine = pl.ds(first, rows)
+    theirs = pl.ds(pl.multiple_of(width - rows - first, rows), rows)
+    to_sibling = remote(panel, sib_own, sib_sem, 0, (sibling, level))
+    to_turn = remote(panel.at[:, mine], turn, turn_sem, 0, (me, level_other))
 
     odd = pair % 2 == 1
     for q in range(CHUNKS):
@@ -162,17 +161,20 @@
     carry_gap = jnp.where(upper, carry_channel, -1.0 - carry_channel)
     edge[2 * bands:, :] = jnp.where(carry_gap >= 0.0, jnp.exp(-jnp.abs(carry_gap) * carry_length), 0.0)
 
-    mine = pl.ds(first, rows)
-    own_split = split(panel[mine, :])
+    own_split = split(panel[...])
     relay(0)
     for kind in range(KINDS):
         grown[kind] = dot3(toeplitz[kind], own_split, NN)
     relay(1)
+    edges = split(edge[...])
+    edges_mine, edges_theirs = split(edge[:, mine]), split(edge[:, theirs])
+    square, aside = split(panel[:, mine]), split(panel[:, theirs])
+    edge_own[:, mine] = dot3(edges_mine, square, NN) + dot3(edges_theirs, aside, NT)
     relay(2)
-    from_turn.wait_recv()
-    edges = split(edge[...])
-    edge_own[...] = dot3(edges, split(panel[...]), NN)
+    edge_own[:, theirs] = dot3(edges_mine, aside, NN)
     relay(3)
+    to_turn.wait_recv()
+    edge_own[:, theirs] = edge_own[:, theirs] + dot3(edges_theirs, split(turn[...]), NN)
     ramps = split(ramp[...])
     place = lax.broadcasted_iota(jnp.int32, (rows, 1), 0)
     reach_in = jnp.where(first == 0, rows - place, place + 1).astype(jnp.float32)
@@ -341,7 +343,8 @@
                 pltpu.VMEM(channel_keep_mask.shape, jnp.int32),
                 pltpu.VMEM(partner_ids.shape, jnp.int32),
                 pltpu.VMEM(band_starts.shape, jnp.int32),
-                pltpu.VMEM((width, width), f32),
+                block,
+                pltpu.VMEM((rows, rows), f32),
                 block, block, block, block, block,
                 pltpu.VMEM((KINDS, rows, rows), bf16),
                 pltpu.VMEM((KINDS, rows, rows), bf16),

time: 42.5 us -> 38.1 us (0.90)
  Pallas kernels: 41 us -> 36.6 us
    pallas_call x1, Pallas kernels: 41 us -> 36.6 us  [body(): pl.pallas_call(partial(kernel, (groups, owners, rows, width, bands)), nam...]
where the time goes in v3:
time: 38.1 us; the launch traced here: 37.9 us
  Pallas kernels  36.6 us (96%)
  local copies, waits for them, and re-layouts  1.3 us (3%)
    pallas_call x1, Pallas kernels, body(): pl.pallas_call(partial(kernel, (groups, owners, rows, width, bands)), nam...  36.6 us
    unnamed x1, local copies, waits for them, and re-layouts  1.3 us

profile of v3, /device:TPU:0, one launch (start us, length us, event | category | flops | bytes accessed | tf_op | source)
XLA Modules:
  0.0 37.9 jit_solution(17281564123245841065)
XLA Ops:
  0.0 36.6 %fisher.1 = f32[2,8,16]{2,1,0:T(8,128)} custom-call(f32[1,256,1024]{2,1,0:T(8,128)} %cov_ref.1, s32[1,1024]{1,0:T(1,128)} %mask_ref.1, s32[1,2]{1,0:T(1,128)} %partner_ref.1, s32[2,64]{1,0:T(2,128)} %starts_ref.1), custom_call_target="tpu_custom_call" | custom-call | tf_op jit(solution)/shard_map/fisher/pallas_call | solution.py:335
  36.6 1.3 %copy.6 = f32[2,16,8]{1,2,0:T(8,128)} copy(f32[2,16,8]{1,2,0:T(8,128)} %bitcast.1) | data formatting | bytes 2048

commit v4 on v3

--- a/solution.py
+++ b/solution.py
@@ -43,8 +43,8 @@
 def kernel(
     sizes, cov_ref, mask_ref, partner_ref, starts_ref, out_ref,
     raw, masks, partner_row, starts, panel, turn, near, far, sib_own, sib_near, sib_far, toep, toep_low, grown, felt,
-    windows, ramp, edge, edge_own, crossed, tiles, landed, share, shares,
-    load_sem, sib_sem, turn_sem, far_sem, near_sem, sfar_sem, snear_sem, fin_send, fin_recv, row_send, row_recv,
+    windows, ramp, edge, edge_own, crossed, tiles, landed,
+    load_sem, sib_sem, turn_sem, far_sem, near_sem, sfar_sem, snear_sem, fin_send, fin_recv, ready,
 ):
     groups, owners, rows, width, bands = sizes
     window = WINDOW_LENGTH
@@ -118,6 +118,8 @@
 
     to_turn.start()
     to_sibling.start()
+    for d in range(1, groups):
+        pl.semaphore_signal(ready, inc=1, device_id=((me + d) % groups, level), device_id_type=MESH)
 
     def relay(q):
         to_far[q].wait_recv()
@@ -262,52 +264,45 @@
     flipped = exact(eye, total, NT) - side[:, 0:bands] - side[:, bands:]
     flipped = flipped * (1.0 / (4 * groups * window))
 
-    for g in range(groups):
-        tiles[g] = flipped[g * tile_rows:(g + 1) * tile_rows, :]
-    landed[pl.ds(me, 1)] = tiles[pl.ds(me, 1)]
+    everyone = groups * owners
+    span = tile_rows * band_share
+    lanes = owners * span
+    source = lax.broadcasted_iota(jnp.int32, (bands, lanes), 0)
+    lane_ids = lax.broadcasted_iota(jnp.int32, (bands, lanes), 1)
+    wanted = lane_ids // span * band_share + lane_ids % band_share
+    repeated = exact(flipped, (source == wanted).astype(jnp.float32), NN)
+    kept = jnp.where(source % tile_rows == lane_ids % span // band_share, repeated, 0.0)
+    gather = lax.broadcasted_iota(jnp.int32, (groups, bands), 1) // tile_rows == lax.broadcasted_iota(
+        jnp.int32, (groups, bands), 0)
+    packed = exact(gather.astype(jnp.float32), kept, NN)
+    for z in range(owners):
+        for g in range(groups):
+            tiles[z * groups + g] = packed[g:g + 1, z * span:(z + 1) * span]
+    here = level * groups + me
+    landed[pl.ds(here, 1)] = tiles[pl.ds(here, 1)]
+    pl.semaphore_wait(ready, groups - 1)
     outgoing = []
-    for d in range(1, groups):
-        peer = (me + d) % groups
+    for d in range(1, everyone):
+        peer = (here + d) % everyone
         copy = pltpu.make_async_remote_copy(
-            src_ref=tiles.at[peer], dst_ref=landed.at[me], send_sem=fin_send.at[peer], recv_sem=fin_recv.at[me],
-            device_id=(peer, level), device_id_type=MESH,
+            src_ref=tiles.at[peer], dst_ref=landed.at[here], send_sem=fin_send.at[peer], recv_sem=fin_recv.at[here],
+            device_id=(peer % groups, peer // groups), device_id_type=MESH,
         )
         copy.start()
         outgoing.append(copy)
-    for d in range(1, groups):
-        peer = (me + d) % groups
+    for d in range(1, everyone):
+        peer = (here + d) % everyone
         pltpu.make_async_remote_copy(
             src_ref=tiles.at[peer], dst_ref=landed.at[peer], send_sem=fin_send.at[peer], recv_sem=fin_recv.at[peer],
-            device_id=(peer, level), device_id_type=MESH,
+            device_id=(peer % groups, peer // groups), device_id_type=MESH,
         ).wait_recv()
-    mine_sum = landed[0]
-    for g in range(1, groups):
-        mine_sum = mine_sum + landed[g]
-    share[...] = mine_sum
-    shares[pl.ds(level, 1)] = mine_sum[None]
-    for d in range(1, owners):
-        peer = (level + d) % owners
-        copy = pltpu.make_async_remote_copy(
-            src_ref=share, dst_ref=shares.at[level], send_sem=row_send.at[peer], recv_sem=row_recv.at[level],
-            device_id=(me, peer), device_id_type=MESH,
-        )
-        copy.start()
-        outgoing.append(copy)
-    for d in range(1, owners):
-        peer = (level + d) % owners
-        pltpu.make_async_remote_copy(
-            src_ref=share, dst_ref=shares.at[peer], send_sem=row_send.at[peer], recv_sem=row_recv.at[peer],
-            device_id=(me, peer), device_id_type=MESH,
-        ).wait_recv()
-    pick = (
-        lax.broadcasted_iota(jnp.int32, (band_share, bands), 0) + level * band_share
-        == lax.broadcasted_iota(jnp.int32, (band_share, bands), 1)
-    ).astype(jnp.float32)
+    row_ids = lax.broadcasted_iota(jnp.int32, (tile_rows, span), 0)
+    keep = row_ids == lax.broadcasted_iota(jnp.int32, (tile_rows, span), 1) // band_share
+    pick = lax.broadcasted_iota(jnp.int32, (span, band_share), 0) % band_share == lax.broadcasted_iota(
+        jnp.int32, (span, band_share), 1)
     for h in range(2):
-        tile = shares[h * per_half]
-        for k in range(1, per_half):
-            tile = tile + shares[h * per_half + k]
-        out_ref[h] = exact(tile, pick, NT)
+        row = jnp.sum(landed[h * everyone // 2:(h + 1) * everyone // 2], axis=0)
+        out_ref[h] = exact(jnp.where(keep, row, 0.0), pick.astype(jnp.float32), NN)
 
     for copy in outgoing:
         copy.wait_send()
@@ -355,13 +350,11 @@
                 pltpu.VMEM((2 * bands + 2 * KINDS, width), f32),
                 pltpu.VMEM((2 * bands + 2 * KINDS, width), f32),
                 pltpu.VMEM((KINDS, 2 * bands, width), f32),
-                pltpu.VMEM((groups, tile_rows, bands), f32),
-                pltpu.VMEM((groups, tile_rows, bands), f32),
-                pltpu.VMEM((tile_rows, bands), f32),
-                pltpu.VMEM((owners, tile_rows, bands), f32),
+                pltpu.VMEM((groups * owners, 1, tile_rows * bands // owners), f32),
+                pltpu.VMEM((groups * owners, 1, tile_rows * bands // owners), f32),
                 dma((4,)), dma((2, 1)), dma((2, 1)),
                 dma((2, CHUNKS)), dma((2, CHUNKS)), dma((2, CHUNKS)), dma((2, CHUNKS)),
-                dma((groups,)), dma((groups,)), dma((owners,)), dma((owners,)),
+                dma((groups * owners,)), dma((groups * owners,)), pltpu.SemaphoreType.REGULAR,
             ],
             compiler_params=pltpu.CompilerParams(
                 collective_id=0, has_side_effects=True, vmem_limit_bytes=67043328

time: 38.1 us -> 37 us (0.971)
  Pallas kernels: 36.6 us -> 35.5 us
    pallas_call x1, Pallas kernels: 36.6 us -> 35.5 us  [body(): pl.pallas_call(partial(kernel, (groups, owners, rows, width, bands)), nam...]
where the time goes in v4:
time: 37 us; the launch traced here: 36.8 us
  Pallas kernels  35.5 us (96%)
  local copies, waits for them, and re-layouts  1.3 us (4%)
    pallas_call x1, Pallas kernels, body(): pl.pallas_call(partial(kernel, (groups, owners, rows, width, bands)), nam...  35.5 us
    unnamed x1, local copies, waits for them, and re-layouts  1.3 us

profile of v4, /device:TPU:0, one launch (start us, length us, event | category | flops | bytes accessed | tf_op | source)
XLA Modules:
  0.0 36.8 jit_solution(4316571976841946647)
XLA Ops:
  0.0 35.5 %fisher.1 = f32[2,8,16]{2,1,0:T(8,128)} custom-call(f32[1,256,1024]{2,1,0:T(8,128)} %cov_ref.1, s32[1,1024]{1,0:T(1,128)} %mask_ref.1, s32[1,2]{1,0:T(1,128)} %partner_ref.1, s32[2,64]{1,0:T(2,128)} %starts_ref.1), custom_call_target="tpu_custom_call" | custom-call | tf_op jit(solution)/shard_map/fisher/pallas_call | solution.py:330
  35.5 1.3 %copy.6 = f32[2,16,8]{1,2,0:T(8,128)} copy(f32[2,16,8]{1,2,0:T(8,128)} %bitcast.1) | data formatting | bytes 2048

commit v5 on v4

--- a/solution.py
+++ b/solution.py
@@ -10,6 +10,7 @@
 WINDOW_LENGTH = 128
 KINDS = 4
 CHUNKS = 8
+PARTS = ((0, 4), (4, 8))
 MESH = pl.DeviceIdType.MESH
 NT = (((1,), (1,)), ((), ()))
 NN = (((1,), (0,)), ((), ()))
@@ -193,9 +194,9 @@
     own_edges = edge_own[0:2 * bands, :]
     across = dot3(split(own_edges), ramps, NT)
     relay(5)
-    middle = CHUNKS // 2
-    for q in range(middle):
+    for q in range(PARTS[0][1]):
         forward(q)
+    relay(6)
     to_sibling.wait_recv()
 
     def weight(baseline):
@@ -209,16 +210,15 @@
     lane = lax.broadcasted_iota(jnp.int32, (1, rows), 1)
 
     def join(part_index, total, chores):
-        span = rows // 2
-        low_row = part_index * span
-        for q in range(part_index * middle, (part_index + 1) * middle):
+        begin, end = PARTS[part_index]
+        span, low_row = (end - begin) * step, begin * step
+        for q in range(begin, end):
             far_on[q].wait_recv()
             near_on[q].wait_recv()
         here = slice(low_row, low_row + span)
         summed = sum(ref[here, :] * factor for ref, factor in weights)
         partners = split(summed)
-        columns = pl.ds(pl.multiple_of(first + low_row, span), span)
-        ramp_here = split(ramp[:, columns])
+        ramp_here = split(ramp[:, mine][:, here])
         leak = dot3(partners, edges, NT)
         leak_bands = leak[:, 0:2 * bands]
         inner = dot3(ramp_here, split(leak_bands), NN)
@@ -239,7 +239,7 @@
             sums = sums + (boxed[0:KINDS * span] + boxed[KINDS * span:])
             found = dot3(ramp_here, split(turned), NN)
             crossed[kind] = found if part_index == 0 else crossed[kind] + found
-        inside_here = windows[KINDS, :, columns]
+        inside_here = windows[KINDS, :, mine][:, here]
         for m in range(KINDS):
             reach = leak_bands * felt[m, here, :]
             high, low = split(sums[m * span:(m + 1) * span] - reach[:, 0:bands] - reach[:, bands:])
@@ -247,12 +247,19 @@
                 band_ids % KINDS == m, dot(inside_here, high, NN) + dot(inside_here, low, NN), 0.0)
         return inner, total
 
-    inner_0, total = join(0, jnp.zeros((bands, bands), jnp.float32), [
-        lambda: relay(6), lambda: relay(7), lambda: forward(4), lambda: forward(5)])
-    for q in range(6, CHUNKS):
-        forward(q)
-    inner_1, total = join(1, total, [])
-    cross = (inner_0 + inner_1) * across
+    done, relayed = PARTS[0][1], 7
+    inner, total = 0.0, jnp.zeros((bands, bands), jnp.float32)
+    for part_index in range(len(PARTS)):
+        chores = []
+        if part_index + 1 < len(PARTS):
+            chores = [partial(relay, q) for q in range(relayed, CHUNKS)]
+            chores += [partial(forward, q) for q in range(done, PARTS[part_index + 1][1])]
+            relayed, done = CHUNKS, PARTS[part_index + 1][1]
+        found, total = join(part_index, total, chores[:KINDS])
+        inner = inner + found
+        for chore in chores[KINDS:]:
+            chore()
+    cross = inner * across
     total = total + cross[0:bands, 0:bands] + cross[0:bands, bands:] + cross[bands:, 0:bands] + cross[bands:, bands:]
     side = jnp.zeros((bands, 2 * bands), jnp.float32)
     for kind in range(KINDS):

time: 37 us -> 36.3 us (0.981)
  Pallas kernels: 35.5 us -> 34.8 us
    pallas_call x1, Pallas kernels: 35.5 us -> 34.8 us  [body(): pl.pallas_call(partial(kernel, (groups, owners, rows, width, bands)), nam...]
where the time goes in v5:
time: 36.3 us; the launch traced here: 36.1 us
  Pallas kernels  34.8 us (96%)
  local copies, waits for them, and re-layouts  1.3 us (4%)
    pallas_call x1, Pallas kernels, body(): pl.pallas_call(partial(kernel, (groups, owners, rows, width, bands)), nam...  34.8 us
    unnamed x1, local copies, waits for them, and re-layouts  1.3 us

profile of v5, /device:TPU:0, one launch (start us, length us, event | category | flops | bytes accessed | tf_op | source)
XLA Modules:
  0.0 36.1 jit_solution(4842643945277608470)
XLA Ops:
  0.0 34.8 %fisher.1 = f32[2,8,16]{2,1,0:T(8,128)} custom-call(f32[1,256,1024]{2,1,0:T(8,128)} %cov_ref.1, s32[1,1024]{1,0:T(1,128)} %mask_ref.1, s32[1,2]{1,0:T(1,128)} %partner_ref.1, s32[2,64]{1,0:T(2,128)} %starts_ref.1), custom_call_target="tpu_custom_call" | custom-call | tf_op jit(solution)/shard_map/fisher/pallas_call | solution.py:337
  34.8 1.3 %copy.6 = f32[2,16,8]{1,2,0:T(8,128)} copy(f32[2,16,8]{1,2,0:T(8,128)} %bitcast.1) | data formatting | bytes 2048
